TPU v7x, 32 devices: a whole 2x2x4 slice. The times are simulated.
32 devices in a mesh: gx: 4 (over x, core), gy: 8 (over z, y).
Axes of the slice: x: 2, y: 2, z: 4, core: 2. Of those that a mesh axis runs over, the one named last changes fastest.
Arguments:
- atm_fields: bfloat16 [196608, 128], P(('gx', 'gy')), may hold values from -6 to 6
- atm_pos: int32 [768], replicated, may hold values from 0 to 767, as said below
- tile_src: int32 [5120], P(('gx', 'gy')), may hold values from 0 to 767, as said below
- tile_tgt: int32 [5120], P(('gx', 'gy')), may hold values from 0 to 1
- tile_count: int32 [32], P(('gx', 'gy')), may hold values from 128 to 160, as said below
- tile_weight: bfloat16 [5120, 256, 256], P(('gx', 'gy')), may hold values from -0.0625 to 0.0625
- ocean_state: bfloat16 [128, 128, 128], P('gy', 'gx'), may hold values from -6 to 6
- land_mask: int32 [128, 128], P('gy', 'gx'), may hold values 0 or 1
- mixing: float32 [128], replicated, may hold values from 0.03 to 0.24
Outputs:
- ocean_next: bfloat16 [128, 128, 128], P('gy', 'gx')
Inputs may be any that keep to these rules, and one draw needn't show every extreme that they name: `atm_pos`: a permutation of the block positions. `tile_src`: among the 160 slots of one device, live or not, no owning device (atm_pos of the block // 24) is named by more than 8 slots; on every device with 160 live slots some owner is named by exactly 8. `tile_count`: live slots are a device's first ones; one device has exactly 160.
All inputs are finite; a program needn't handle non-finite values. No bound on the sum of `land_mask` on one device may be relied on, other than what follows from the above.
Results may differ from a plain program's by a relative error of at most 0.001.
Values may be sent and summed in bfloat16 or wider, within the bound.
No kernel may reach another device: no remote copies, remote signals or barrier semaphores. Data moves between devices by JAX's collectives and lax.ppermute only.
A program may use at most 128 MiB of HBM per device.

v0:
```python
import jax
import jax.numpy as jnp
from jax import lax
from jax.sharding import PartitionSpec as P

RECV_SLOTS = 256


def padded(shard, sides, width, wrap):
    for axis, dim in sides:
        size, length = (lax.axis_size(axis), shard.shape[dim])
        up = [(i, (i + 1) % size) for i in range(size if wrap else size - 1)]
        down = [(j, i) for i, j in up]
        last = lax.slice_in_dim(shard, length - width, length, axis=dim)
        leading = lax.slice_in_dim(shard, 0, width, axis=dim)
        before = lax.ppermute(last, axis, up)
        after = lax.ppermute(leading, axis, down)
        shard = jnp.concatenate([before, shard, after], axis=dim)
    return shard


def partner(value, axis, distance):
    mask = 2**distance
    pairs = [(source, source ^ mask) for source in range(lax.axis_size(axis))]
    return lax.ppermute(value, axis, pairs)


def plan_tiles(sources, tile_live, atm_pos, block_count):
    positions = atm_pos[sources]
    owners = positions // block_count
    local_slot = positions % block_count
    ordinal = jnp.arange(sources.shape[0], dtype=jnp.int32)
    active = ordinal < tile_live
    earlier = (
        (owners[:, None] == owners[None, :])
        & active[None, :]
        & (ordinal[None, :] < ordinal[:, None])
    )
    order_rank = jnp.sum(earlier.astype(jnp.int32), axis=1)
    return (owners, order_rank, local_slot, active)


def local(
    atm_fields, atm_pos, tile_src, tile_tgt, tile_count, tile_weight, ocean_state, land_mask, mixing
):
    block_rows = tile_weight.shape[1]
    tiles = tile_weight.shape[0]
    channels = atm_fields.shape[1]
    block_count = atm_fields.shape[0] // block_rows
    devices = lax.axis_size("gx") * lax.axis_size("gy")
    per_peer = RECV_SLOTS // devices
    owners, order_rank, local_slot, active = plan_tiles(
        tile_src, tile_count[0], atm_pos, block_count
    )
    slots_flat = jnp.arange(RECV_SLOTS, dtype=jnp.int32)
    wanted_slot = owners * per_peer + order_rank
    matches = (wanted_slot[None, :] == slots_flat[:, None]) & active[None, :]
    asking = jnp.sum(jnp.where(matches, local_slot[None, :] + 1, 0), axis=1)
    requests = lax.all_to_all(
        asking.reshape(devices, per_peer), ("gx", "gy"), split_axis=0, concat_axis=0, tiled=True
    )
    wanted = requests.reshape(RECV_SLOTS)
    block_table = atm_fields.reshape(block_count, block_rows, channels)
    outgoing = jnp.where(
        (wanted > 0)[:, None, None],
        block_table[jnp.maximum(wanted - 1, 0)],
        jnp.zeros((), jnp.bfloat16),
    )
    outgoing = outgoing.reshape(devices, per_peer, block_rows, channels)
    arrived = lax.all_to_all(outgoing, ("gx", "gy"), split_axis=0, concat_axis=0, tiled=True)
    arrived = arrived.reshape(RECV_SLOTS, block_rows, channels)
    lat_rows = ocean_state.shape[0]
    lon_cols = ocean_state.shape[1]
    target_blocks = lat_rows * lon_cols // block_rows
    slots = jnp.where(active, owners * per_peer + order_rank, 0)
    select = (
        (tile_tgt[:, None] == jnp.arange(target_blocks, dtype=jnp.int32)[None, :]) & active[:, None]
    ).astype(jnp.float32)
    group_size = max((divisor for divisor in range(1, 33) if tiles % divisor == 0))
    groups = tiles // group_size

    def advance(running, pieces):
        weights, group_slots, group_select = pieces
        gathered = arrived[group_slots]
        partial_sum = jnp.einsum(
            "tij,tjc->tic", weights, gathered, preferred_element_type=jnp.float32
        )
        added = jnp.einsum(
            "tb,tic->bic", group_select, partial_sum, precision=lax.Precision.HIGHEST
        )
        return (running + added, None)

    starting = jnp.zeros((target_blocks, block_rows, channels), jnp.float32)
    remapped = lax.scan(
        advance,
        starting,
        (
            tile_weight.reshape(groups, group_size, block_rows, block_rows),
            slots.reshape(groups, group_size),
            select.reshape(groups, group_size, target_blocks),
        ),
    )[0]
    forcing = remapped.reshape(lat_rows, lon_cols, channels)
    mask_half = land_mask.astype(jnp.bfloat16)
    lon_state, lon_mask = (
        padded(ocean_state, (("gx", 1),), 1, True),
        padded(mask_half, (("gx", 1),), 1, True),
    )
    lat_state, lat_mask = (
        padded(ocean_state, (("gy", 0),), 1, False),
        padded(mask_half, (("gy", 0),), 1, False),
    )
    fold_state = jnp.flip(ocean_state[-1], 0)
    fold_mask = jnp.flip(mask_half[-1], 0)
    for bit_number in range(lax.axis_size("gx").bit_length() - 1):
        fold_state, fold_mask = partner((fold_state, fold_mask), "gx", bit_number)
    is_top = lax.axis_index("gy") == lax.axis_size("gy") - 1
    north_state = jnp.concatenate(
        [lat_state[2:-1], jnp.where(is_top, fold_state, lat_state[-1])[None]], axis=0
    )
    north_mask = jnp.concatenate(
        [lat_mask[2:-1], jnp.where(is_top, fold_mask, lat_mask[-1])[None]], axis=0
    )
    center = ocean_state.astype(jnp.float32)
    sides = (
        (lon_state[:, :-2], lon_mask[:, :-2]),
        (lon_state[:, 2:], lon_mask[:, 2:]),
        (lat_state[:-2], lat_mask[:-2]),
        (north_state, north_mask),
    )
    diffusion = jnp.zeros_like(center)
    for side_state, side_mask in sides:
        diffusion = diffusion + side_mask.astype(jnp.float32)[..., None] * (
            side_state.astype(jnp.float32) - center
        )
    result = mask_half.astype(jnp.float32)[..., None] * (center + forcing + mixing * diffusion)
    return result.astype(jnp.bfloat16)


def solution(mesh):
    in_specs = (
        P(("gx", "gy"), None),
        P(),
        P(("gx", "gy")),
        P(("gx", "gy")),
        P(("gx", "gy")),
        P(("gx", "gy"), None, None),
        P("gy", "gx", None),
        P("gy", "gx"),
        P(),
    )
    out_specs = P("gy", "gx", None)
    return jax.shard_map(local, mesh=mesh, in_specs=in_specs, out_specs=out_specs, check_vma=False)
```

profile of v0, /device:TPU:0, one launch (start us, length us, event | category | flops | bytes accessed | tf_op | source)
XLA Modules:
  0.0 530.6 jit_solution(13678297250485912902)
XLA Ops:
  0.8 1.9 gather_fusion.1
  3.9 14.3 %all_to_all.14 = s32[32,1,8]{2,1,0:T(1,128)S(1)} all-to-all(s32[32,1,8]{2,1,0:T(1,128)S(1)} %bitcast.58), channel_id=1, replica_groups=mesh['gx'=4,'gy'=8] {'gx','gy'}, dimensions={0} | all-to-all | bytes 2048 | tf_op jit(solution)/shard_map/all_to_all | solution.py:59
  18.5 9.6 %gather_fusion.2 = bf16[256,256,128]{2,1,0:T(8,128)(2,1)} fusion(bf16[24,256,128]{2,1,0:T(8,128)(2,1)S(1)} %bitcast.54, s32[1024]{0:T(1024)S(1)} %pad_clamp_fusion.1), kind=kCustom, calls=%fused_computation.2 | custom fusion | bytes 33555456 | tf_op jit(solution)/shard_map/gather | solution.py:66
  28.1 14.0 %broadcast_select_fusion = bf16[32,8,256,128]{3,2,1,0:T(8,128)(2,1)} fusion(bf16[32,8,256,128]{3,2,1,0:T(8,128)(2,1)} %bitcast.55, pred[32,8]{1,0:T(8,128)(4,1)S(1)} %copy.25), kind=kLoop, calls=%fused_computation.18 | loop fusion | flops 8388608 | bytes 33554688 | tf_op jit(solution)/shard_map/jit(_where)/select_n | solution.py:64
  42.1 4.0 all-to-all-start.1
  46.2 3.5 collective-permute-start.4
  49.7 1.7 collective-permute-start.2
  51.6 1.3 collective-permute-start.8
  53.3 87.1 %collective-permute-done = bf16[16,1]{1,0:T(8,128)(2,1)S(1)} collective-permute-done((bf16[16,1]{1,0:T(8,128)(2,1)S(1)}, bf16[16,1]{1,0:T(8,128)(2,1)S(1)}, u32[]{:S(2)}, u32[]{:S(2)}) %collective-permute-start) | collective-permute-done | bytes 64 | tf_op jit(solution)/shard_map/ppermute | solution.py:16
  140.5 1.3 collective-permute-start.11
  141.8 197.8 %collective-permute-start.5 = (bf16[1,32,128]{2,1,0:T(8,128)(2,1)S(1)}, bf16[1,32,128]{2,1,0:T(8,128)(2,1)S(1)}, u32[]{:S(2)}, u32[]{:S(2)}) collective-permute-start(bf16[1,32,128]{2,1,0:T(8,128)(2,1)S(1)} %get-tuple-element.78), channel_id=1, source_target_pairs={{0,1},{1,2},{2,3},{3,4},{4,5},{5,6},{6,7},{8,9},{9,10},{10,11},{11... | collective-permute-start | bytes 24584 | tf_op jit(solution)/shard_map/ppermute | solution.py:16
  339.6 0.9 collective-permute-start.7
  340.5 2.7 collective-permute-done.7
  344.1 2.8 collective-permute-done.10
  346.9 74.2 %all-to-all-done.1 = bf16[32,8,256,128]{3,2,1,0:T(8,128)(2,1)} async-done(((bf16[32,8,256,128]{3,2,1,0:T(8,128)(2,1)}), bf16[32,8,256,128]{3,2,1,0:T(8,128)(2,1)}, u32[]{:S(2)}, u32[]{:S(2)}) %all-to-all-start.1) | async-done | bytes 16777248 | tf_op jit(solution)/shard_map/all_to_all | solution.py:70
  421.2 108.0 %while.11 = (s32[]{:T(128)}, f32[2,256,128]{2,0,1:T(2,128)S(1)}, f32[5,32,2]{1,2,0:T(2,128)S(1)}, bf16[5,32,256,256]{3,2,1,0:T(8,128)(2,1)}, s32[5,32]{1,0:T(8,1...) while((s32[]{:T(128)}, f32[2,256,128]{2,0,1:T(2,128)S(1)}, ...), condition=%wide.region_3.4_spmd.clone, body=%wide.region_2.3_spmd.clone.sunk | while | flops 562168960 | bytes 19404904 | solution.py:94
  421.2 8.0 %gather_fusion = bf16[32,256,128]{2,1,0:T(8,128)(2,1)} fusion(bf16[256,256,128]{2,1,0:T(8,128)(2,1)} %get-tuple-element.148, s32[1024]{0:T(1024)S(1)} %pad_clamp_fusion.4), kind=kCustom, calls=%fused_computation.clone.clone.1 | custom fusion | bytes 4194432 | tf_op jit(solution)/shard_map/while/body/eval_jaxpr/gather | solution.py:84
  429.2 6.0 %fusion.54 = f32[32,256,128]{2,1,0:T(8,128)} fusion(bf16[32,256,128]{2,1,0:T(8,128)(2,1)} %gather_fusion, bf16[5,32,256,256]{3,2,1,0:T(8,128)(2,1)} %get-tuple-element.146, s32[]{:T(128)} %get-tuple-element.135), kind=kOutput, calls=%fused_computation.3.clone.1 | convolution fusion | flops 536870912 | bytes 10486272 | tf_op jit(solution)/shard_map/while/body/eval_jaxpr/tij,tjc->tic/dot_general | solution.py:85
  435.2 7.6 %fusion.55 = f32[2,256,128]{2,0,1:T(2,128)S(1)} fusion(f32[32,256,128]{2,1,0:T(8,128)} %fusion.54, f32[2,256,128]{2,0,1:T(2,128)S(1)} %get-tuple-element.136, pred[]{:T(512)S(6)} %compare.3, f32[5,32,2]{1,2,0:T(2,128)S(1)} %get-tuple-element.145, s32[]{:T(128)} %get-tuple-element.135), kind=kOutput, calls=%fused_computation.8.clone.1 | convolution fusion | flops 25296896 | bytes 4719621 | tf_op jit(solution)/shard_map/while/body/eval_jaxpr/tb,tic->bic/dot_general | solution.py:88
  442.8 7.9 %gather_fusion = bf16[32,256,128]{2,1,0:T(8,128)(2,1)} fusion(bf16[256,256,128]{2,1,0:T(8,128)(2,1)} %get-tuple-element.148, s32[1024]{0:T(1024)S(1)} %pad_clamp_fusion.4), kind=kCustom, calls=%fused_computation.clone.clone.1 | custom fusion | bytes 4194432 | tf_op jit(solution)/shard_map/while/body/eval_jaxpr/gather | solution.py:84
  450.8 6.0 %fusion.54 = f32[32,256,128]{2,1,0:T(8,128)} fusion(bf16[32,256,128]{2,1,0:T(8,128)(2,1)} %gather_fusion, bf16[5,32,256,256]{3,2,1,0:T(8,128)(2,1)} %get-tuple-element.146, s32[]{:T(128)} %get-tuple-element.135), kind=kOutput, calls=%fused_computation.3.clone.1 | convolution fusion | flops 536870912 | bytes 10486272 | tf_op jit(solution)/shard_map/while/body/eval_jaxpr/tij,tjc->tic/dot_general | solution.py:85
  456.8 7.6 %fusion.55 = f32[2,256,128]{2,0,1:T(2,128)S(1)} fusion(f32[32,256,128]{2,1,0:T(8,128)} %fusion.54, f32[2,256,128]{2,0,1:T(2,128)S(1)} %get-tuple-element.136, pred[]{:T(512)S(6)} %compare.3, f32[5,32,2]{1,2,0:T(2,128)S(1)} %get-tuple-element.145, s32[]{:T(128)} %get-tuple-element.135), kind=kOutput, calls=%fused_computation.8.clone.1 | convolution fusion | flops 25296896 | bytes 4719621 | tf_op jit(solution)/shard_map/while/body/eval_jaxpr/tb,tic->bic/dot_general | solution.py:88
  464.4 7.9 %gather_fusion = bf16[32,256,128]{2,1,0:T(8,128)(2,1)} fusion(bf16[256,256,128]{2,1,0:T(8,128)(2,1)} %get-tuple-element.148, s32[1024]{0:T(1024)S(1)} %pad_clamp_fusion.4), kind=kCustom, calls=%fused_computation.clone.clone.1 | custom fusion | bytes 4194432 | tf_op jit(solution)/shard_map/while/body/eval_jaxpr/gather | solution.py:84
  472.4 6.0 %fusion.54 = f32[32,256,128]{2,1,0:T(8,128)} fusion(bf16[32,256,128]{2,1,0:T(8,128)(2,1)} %gather_fusion, bf16[5,32,256,256]{3,2,1,0:T(8,128)(2,1)} %get-tuple-element.146, s32[]{:T(128)} %get-tuple-element.135), kind=kOutput, calls=%fused_computation.3.clone.1 | convolution fusion | flops 536870912 | bytes 10486272 | tf_op jit(solution)/shard_map/while/body/eval_jaxpr/tij,tjc->tic/dot_general | solution.py:85
  478.4 7.6 %fusion.55 = f32[2,256,128]{2,0,1:T(2,128)S(1)} fusion(f32[32,256,128]{2,1,0:T(8,128)} %fusion.54, f32[2,256,128]{2,0,1:T(2,128)S(1)} %get-tuple-element.136, pred[]{:T(512)S(6)} %compare.3, f32[5,32,2]{1,2,0:T(2,128)S(1)} %get-tuple-element.145, s32[]{:T(128)} %get-tuple-element.135), kind=kOutput, calls=%fused_computation.8.clone.1 | convolution fusion | flops 25296896 | bytes 4719621 | tf_op jit(solution)/shard_map/while/body/eval_jaxpr/tb,tic->bic/dot_general | solution.py:88
  486.0 7.9 %gather_fusion = bf16[32,256,128]{2,1,0:T(8,128)(2,1)} fusion(bf16[256,256,128]{2,1,0:T(8,128)(2,1)} %get-tuple-element.148, s32[1024]{0:T(1024)S(1)} %pad_clamp_fusion.4), kind=kCustom, calls=%fused_computation.clone.clone.1 | custom fusion | bytes 4194432 | tf_op jit(solution)/shard_map/while/body/eval_jaxpr/gather | solution.py:84
  493.9 6.0 %fusion.54 = f32[32,256,128]{2,1,0:T(8,128)} fusion(bf16[32,256,128]{2,1,0:T(8,128)(2,1)} %gather_fusion, bf16[5,32,256,256]{3,2,1,0:T(8,128)(2,1)} %get-tuple-element.146, s32[]{:T(128)} %get-tuple-element.135), kind=kOutput, calls=%fused_computation.3.clone.1 | convolution fusion | flops 536870912 | bytes 10486272 | tf_op jit(solution)/shard_map/while/body/eval_jaxpr/tij,tjc->tic/dot_general | solution.py:85
  500.0 7.6 %fusion.55 = f32[2,256,128]{2,0,1:T(2,128)S(1)} fusion(f32[32,256,128]{2,1,0:T(8,128)} %fusion.54, f32[2,256,128]{2,0,1:T(2,128)S(1)} %get-tuple-element.136, pred[]{:T(512)S(6)} %compare.3, f32[5,32,2]{1,2,0:T(2,128)S(1)} %get-tuple-element.145, s32[]{:T(128)} %get-tuple-element.135), kind=kOutput, calls=%fused_computation.8.clone.1 | convolution fusion | flops 25296896 | bytes 4719621 | tf_op jit(solution)/shard_map/while/body/eval_jaxpr/tb,tic->bic/dot_general | solution.py:88
  507.6 7.9 %gather_fusion = bf16[32,256,128]{2,1,0:T(8,128)(2,1)} fusion(bf16[256,256,128]{2,1,0:T(8,128)(2,1)} %get-tuple-element.148, s32[1024]{0:T(1024)S(1)} %pad_clamp_fusion.4), kind=kCustom, calls=%fused_computation.clone.clone.1 | custom fusion | bytes 4194432 | tf_op jit(solution)/shard_map/while/body/eval_jaxpr/gather | solution.py:84
  515.5 6.0 %fusion.54 = f32[32,256,128]{2,1,0:T(8,128)} fusion(bf16[32,256,128]{2,1,0:T(8,128)(2,1)} %gather_fusion, bf16[5,32,256,256]{3,2,1,0:T(8,128)(2,1)} %get-tuple-element.146, s32[]{:T(128)} %get-tuple-element.135), kind=kOutput, calls=%fused_computation.3.clone.1 | convolution fusion | flops 536870912 | bytes 10486272 | tf_op jit(solution)/shard_map/while/body/eval_jaxpr/tij,tjc->tic/dot_general | solution.py:85
  521.6 7.6 %fusion.55 = f32[2,256,128]{2,0,1:T(2,128)S(1)} fusion(f32[32,256,128]{2,1,0:T(8,128)} %fusion.54, f32[2,256,128]{2,0,1:T(2,128)S(1)} %get-tuple-element.136, pred[]{:T(512)S(6)} %compare.3, f32[5,32,2]{1,2,0:T(2,128)S(1)} %get-tuple-element.145, s32[]{:T(128)} %get-tuple-element.135), kind=kOutput, calls=%fused_computation.8.clone.1 | convolution fusion | flops 25296896 | bytes 4719621 | tf_op jit(solution)/shard_map/while/body/eval_jaxpr/tb,tic->bic/dot_general | solution.py:88
  529.3 1.1 fusion.16
  (77 shorter events, 3.6 us)
Async XLA Ops:
  0.0 18.5 %copy-start = (bf16[6144,128]{1,0:T(8,128)(2,1)S(1)}, bf16[6144,128]{1,0:T(8,128)(2,1)}, u32[]{:S(2)}) copy-start(bf16[6144,128]{1,0:T(8,128)(2,1)} %param.11) | copy-start | bytes 4718596
  42.1 4.1 copy-start.4
  42.1 11.0 %copy-start.5 = (s32[160]{0:T(256)S(1)}, s32[160]{0:T(256)}, u32[]{:S(2)}) copy-start(s32[160]{0:T(256)} %param.14) | copy-start | bytes 1924
  42.1 11.1 %copy-start.2 = (bf16[16,32,128]{2,1,0:T(8,128)(2,1)S(1)}, bf16[16,32,128]{2,1,0:T(8,128)(2,1)}, u32[]{:S(2)}) copy-start(bf16[16,32,128]{2,1,0:T(8,128)(2,1)} %param.17) | copy-start | bytes 393220
  42.1 379.1 %all-to-all-start.1 = ((bf16[32,8,256,128]{3,2,1,0:T(8,128)(2,1)}), bf16[32,8,256,128]{3,2,1,0:T(8,128)(2,1)}, u32[]{:S(2)}, u32[]{:S(2)}) async-start(bf16[32,8,256,128]{3,2,1,0:T(8,128)(2,1)} %broadcast_select_fusion), calls=%async_computation.1 | async-start | bytes 33554432 | tf_op jit(solution)/shard_map/all_to_all | solution.py:70
  46.2 95.6 %collective-permute-start.4 = (bf16[1,32]{1,0:T(2,128)(2,1)S(1)}, bf16[1,32]{1,0:T(2,128)(2,1)S(1)}, u32[]{:S(2)}, u32[]{:S(2)}) collective-permute-start(bf16[1,32]{1,0:T(2,128)(2,1)S(1)} %get-tuple-element.86), channel_id=1, source_target_pairs={{0,1},{1,2},{2,3},{3,4},{4,5},{5,6},{6,7},{8,9},{9,10},{10,11},{11... | collective-permute-start | bytes 200 | tf_op jit(solution)/shard_map/ppermute | solution.py:16
  49.7 90.7 %collective-permute-start = (bf16[16,1]{1,0:T(8,128)(2,1)S(1)}, bf16[16,1]{1,0:T(8,128)(2,1)S(1)}, u32[]{:S(2)}, u32[]{:S(2)}) collective-permute-start(bf16[16,1]{1,0:T(8,128)(2,1)S(1)} %get-tuple-element.84), channel_id=1, source_target_pairs={{0,8},{8,16},{16,24},{24,0},{1,9},{9,17},{17,25},{25,1},{2,10},{10... | collective-permute-start | bytes 104 | tf_op jit(solution)/shard_map/ppermute | solution.py:16
  49.7 90.7 %collective-permute-start.2 = (bf16[16,1]{1,0:T(8,128)(2,1)S(1)}, bf16[16,1]{1,0:T(8,128)(2,1)S(1)}, u32[]{:S(2)}, u32[]{:S(2)}) collective-permute-start(bf16[16,1]{1,0:T(8,128)(2,1)S(1)} %get-tuple-element.85), channel_id=1, source_target_pairs={{8,0},{16,8},{24,16},{0,24},{9,1},{17,9},{25,17},{1,25},{10,2},{18... | collective-permute-start | bytes 104 | tf_op jit(solution)/shard_map/ppermute | solution.py:17
  51.6 288.0 %collective-permute-start.6 = (bf16[32]{0:T(256)(128)(2,1)S(1)}, bf16[32]{0:T(256)(128)(2,1)S(1)}, u32[]{:S(2)}, u32[]{:S(2)}) collective-permute-start(bf16[32]{0:T(256)(128)(2,1)S(1)} %rev.8), channel_id=1, source_target_pairs={{0,8},{8,0},{16,24},{24,16},{1,9},{9,1},{17,25},{25,17},{2,10},{10... | collective-permute-start | bytes 200 | tf_op jit(solution)/shard_map/ppermute | solution.py:25
  51.6 288.9 %collective-permute-start.8 = (bf16[1,32]{1,0:T(2,128)(2,1)S(1)}, bf16[1,32]{1,0:T(2,128)(2,1)S(1)}, u32[]{:S(2)}, u32[]{:S(2)}) collective-permute-start(bf16[1,32]{1,0:T(2,128)(2,1)S(1)} %get-tuple-element.87), channel_id=1, source_target_pairs={{1,0},{2,1},{3,2},{4,3},{5,4},{6,5},{7,6},{9,8},{10,9},{11,10},{12... | collective-permute-start | bytes 200 | tf_op jit(solution)/shard_map/ppermute | solution.py:17
  140.5 202.8 %collective-permute-start.9 = (bf16[32,128]{1,0:T(8,128)(2,1)S(1)}, bf16[32,128]{1,0:T(8,128)(2,1)S(1)}, u32[]{:S(2)}, u32[]{:S(2)}) collective-permute-start(bf16[32,128]{1,0:T(8,128)(2,1)S(1)} %rev.9), channel_id=1, source_target_pairs={{0,8},{8,0},{16,24},{24,16},{1,9},{9,1},{17,25},{25,17},{2,10},{10... | collective-permute-start | bytes 24584 | tf_op jit(solution)/shard_map/ppermute | solution.py:25
  140.5 203.6 %collective-permute-start.11 = (bf16[1,32,128]{2,1,0:T(8,128)(2,1)S(1)}, bf16[1,32,128]{2,1,0:T(8,128)(2,1)S(1)}, u32[]{:S(2)}, u32[]{:S(2)}) collective-permute-start(bf16[1,32,128]{2,1,0:T(8,128)(2,1)S(1)} %get-tuple-element.76), channel_id=1, source_target_pairs={{1,0},{2,1},{3,2},{4,3},{5,4},{6,5},{7,6},{9,8},{10,9},{11,10},{12... | collective-permute-start | bytes 24584 | tf_op jit(solution)/shard_map/ppermute | solution.py:17
  141.8 387.4 %collective-permute-start.5 = (bf16[1,32,128]{2,1,0:T(8,128)(2,1)S(1)}, bf16[1,32,128]{2,1,0:T(8,128)(2,1)S(1)}, u32[]{:S(2)}, u32[]{:S(2)}) collective-permute-start(bf16[1,32,128]{2,1,0:T(8,128)(2,1)S(1)} %get-tuple-element.78), channel_id=1, source_target_pairs={{0,1},{1,2},{2,3},{3,4},{4,5},{5,6},{6,7},{8,9},{9,10},{10,11},{11... | collective-permute-start | bytes 24584 | tf_op jit(solution)/shard_map/ppermute | solution.py:16
  339.6 3.6 collective-permute-start.7
  340.5 188.7 %collective-permute-start.1 = (bf16[16,1,128]{2,1,0:T(2,128)(2,1)S(1)}, bf16[16,1,128]{2,1,0:T(2,128)(2,1)S(1)}, u32[]{:S(2)}, u32[]{:S(2)}) collective-permute-start(bf16[16,1,128]{2,1,0:T(2,128)(2,1)S(1)} %get-tuple-element.79), channel_id=1, source_target_pairs={{0,8},{8,16},{16,24},{24,0},{1,9},{9,17},{17,25},{25,1},{2,10},{10... | collective-permute-start | bytes 12296 | tf_op jit(solution)/shard_map/ppermute | solution.py:16
  343.2 186.0 %collective-permute-start.3 = (bf16[16,1,128]{2,1,0:T(2,128)(2,1)S(1)}, bf16[16,1,128]{2,1,0:T(2,128)(2,1)S(1)}, u32[]{:S(2)}, u32[]{:S(2)}) collective-permute-start(bf16[16,1,128]{2,1,0:T(2,128)(2,1)S(1)} %get-tuple-element.80), channel_id=1, source_target_pairs={{8,0},{16,8},{24,16},{0,24},{9,1},{17,9},{25,17},{1,25},{10,2},{18... | collective-permute-start | bytes 12296 | tf_op jit(solution)/shard_map/ppermute | solution.py:17
  343.2 3.7 collective-permute-start.10
  421.2 108.1 %copy-start.3 = (bf16[16,32,128]{2,1,0:T(8,128)(2,1)S(1)}, bf16[16,32,128]{2,1,0:T(8,128)(2,1)}, u32[]{:S(2)}) copy-start(bf16[16,32,128]{2,1,0:T(8,128)(2,1)} %param.17) | copy-start | bytes 393220
  421.2 108.1 %slice-start = ((bf16[16,32,128]{2,1,0:T(8,128)(2,1)}), bf16[15,32,128]{2,1,0:T(8,128)(2,1)S(1)}, s32[]{:S(2)}) async-start(bf16[16,32,128]{2,1,0:T(8,128)(2,1)} %param.17), calls=%async_computation.2 | async-start | bytes 245760 | tf_op jit(solution)/shard_map/slice | solution.py:119
  421.2 108.1 %copy-start.6 = (f32[128]{0:T(128)S(1)}, f32[128]{0:T(128)}, u32[]{:S(2)}) copy-start(f32[128]{0:T(128)} %param.19) | copy-start | bytes 1540
  529.2 1.4 copy-start.1
where the time goes:
time: 531 us
  starting transfers between devices  211 us (40%)
  waiting for transfers between devices  167 us (31%)
  matrix products  68.1 us (13%)
  local copies, waits for them, and re-layouts  52.5 us (10%)
  other arithmetic  16.5 us (3%)
  blocking collectives  14.3 us (3%)
    ppermute x4, starting transfers between devices, padded(): before = lax.ppermute(last, axis, up)  201 us
    ppermute x4, waiting for transfers between devices, padded(): before = lax.ppermute(last, axis, up)  87.2 us
    all_to_all x1, waiting for transfers between devices, local(): lax.all_to_all(outgoing, ('gx', 'gy'), split_axis=0, concat_axis=0, tiled...  74.2 us
    gather x5, local copies, waits for them, and re-layouts, advance(): gathered = arrived[group_slots]  39.7 us
    dot_general x5, matrix products, advance(): jnp.einsum('tb,tic->bic', group_select, partial_sum, precision=lax.Precis...  37.8 us
    dot_general x5, matrix products, advance(): jnp.einsum('tij,tjc->tic', weights, gathered, preferred_element_type=jnp....  30.2 us
    all_to_all x1, blocking collectives, local(): lax.all_to_all(asking.reshape(devices, per_peer), ('gx', 'gy'), split_axi...  14.3 us
    select_n x1, other arithmetic, local(): jnp.where((wanted > 0)[:, None, None], block_table[jnp.maximum(wanted - 1...  14 us
  transfers between devices with their start and end apart: 13, of which 4 were waited for; matrix products, arithmetic and copies ran while one was open for 20% of the time, Pallas kernels for 0%

commit v1 on v0

--- a/solution.py
+++ b/solution.py
@@ -1,9 +1,82 @@
 import jax
 import jax.numpy as jnp
 from jax import lax
+from jax.experimental import pallas as pl
+from jax.experimental.pallas import tpu as pltpu
 from jax.sharding import PartitionSpec as P
 
 RECV_SLOTS = 256
+
+STEP_TILES = 10
+GATHER_LIMIT = 64 * 2**20
+
+
+def tile_kernel(starts, place, target, weights, *refs):
+    buffers, out, blocks, sems = refs[: len(starts)], refs[-3], refs[-2], refs[-1]
+    group = weights.shape[0]
+    step = pl.program_id(0)
+    steps = pl.num_programs(0)
+
+    def issue(at, slot):
+        for j in range(group):
+            where = place[at * group + j]
+            for n, buffer in enumerate(buffers):
+                first = starts[n]
+                last = first + buffer.shape[0]
+
+                @pl.when((where >= first) & (where < last))
+                def _():
+                    pltpu.make_async_copy(
+                        buffer.at[where - first], blocks.at[slot, j], sems.at[slot, j]
+                    ).start()
+
+    @pl.when(step == 0)
+    def _():
+        out[...] = jnp.zeros_like(out)
+        issue(0, 0)
+
+    @pl.when(step + 1 < steps)
+    def _():
+        issue(step + 1, (step + 1) % 2)
+
+    slot = step % 2
+    for j in range(group):
+        pltpu.make_async_copy(buffers[0].at[0], blocks.at[slot, j], sems.at[slot, j]).wait()
+    for j in range(group):
+        at = target[step * group + j]
+        out[at] += jnp.dot(weights[j], blocks[slot, j], preferred_element_type=jnp.float32)
+
+
+def remap(place, target, tile_weight, buffers, target_blocks):
+    tiles, block_rows, _ = tile_weight.shape
+    channels = buffers[0].shape[-1]
+    group = max(d for d in range(1, STEP_TILES + 1) if tiles % d == 0)
+    starts = []
+    total = 0
+    for buffer in buffers:
+        starts.append(total)
+        total += buffer.shape[0]
+
+    def body(place_ref, target_ref, weights, *refs):
+        tile_kernel(starts, place_ref, target_ref, weights, *refs)
+
+    result = pl.pallas_call(
+        body,
+        grid_spec=pltpu.PrefetchScalarGridSpec(
+            num_scalar_prefetch=2,
+            grid=(tiles // group,),
+            in_specs=[pl.BlockSpec((group, block_rows, block_rows), lambda i, *_: (i, 0, 0))]
+            + [pl.BlockSpec(memory_space=pl.ANY)] * len(buffers),
+            out_specs=pl.BlockSpec((target_blocks + 1, block_rows, channels), lambda i, *_: (0, 0, 0)),
+            scratch_shapes=[
+                pltpu.VMEM((2, group, block_rows, channels), jnp.bfloat16),
+                pltpu.SemaphoreType.DMA((2, group)),
+            ],
+        ),
+        out_shape=jax.ShapeDtypeStruct((target_blocks + 1, block_rows, channels), jnp.float32),
+        compiler_params=pltpu.CompilerParams(dimension_semantics=("arbitrary",)),
+    )(place, target, tile_weight, *buffers)
+    return result[:target_blocks]
 
 
 def padded(shard, sides, width, wrap):
@@ -40,6 +113,29 @@
     return (owners, order_rank, local_slot, active)
 
 
+def exchanged_blocks(block_table, tile_src, tile_live, atm_pos):
+    block_count, block_rows, channels = block_table.shape
+    devices = lax.axis_size("gx") * lax.axis_size("gy")
+    per_peer = RECV_SLOTS // devices
+    owners, order_rank, local_slot, active = plan_tiles(tile_src, tile_live, atm_pos, block_count)
+    slots_flat = jnp.arange(RECV_SLOTS, dtype=jnp.int32)
+    wanted_slot = owners * per_peer + order_rank
+    matches = (wanted_slot[None, :] == slots_flat[:, None]) & active[None, :]
+    asking = jnp.sum(jnp.where(matches, local_slot[None, :], 0), axis=1)
+    requests = lax.all_to_all(
+        asking.reshape(devices, per_peer), ("gx", "gy"), split_axis=0, concat_axis=0, tiled=True
+    )
+    outgoing = block_table[requests.reshape(RECV_SLOTS)]
+    outgoing = outgoing.reshape(devices, per_peer, block_rows, channels)
+    arrived = lax.all_to_all(outgoing, ("gx", "gy"), split_axis=0, concat_axis=0, tiled=True)
+    arrived = arrived.reshape(RECV_SLOTS, block_rows, channels)
+    return jnp.where(active, wanted_slot, 0), [arrived]
+
+
+def gathered_blocks(block_table, positions):
+    return positions, [lax.all_gather(block_table, ("gx", "gy"), tiled=True)]
+
+
 def local(
     atm_fields, atm_pos, tile_src, tile_tgt, tile_count, tile_weight, ocean_state, land_mask, mixing
 ):
@@ -48,58 +144,17 @@
     channels = atm_fields.shape[1]
     block_count = atm_fields.shape[0] // block_rows
     devices = lax.axis_size("gx") * lax.axis_size("gy")
-    per_peer = RECV_SLOTS // devices
-    owners, order_rank, local_slot, active = plan_tiles(
-        tile_src, tile_count[0], atm_pos, block_count
-    )
-    slots_flat = jnp.arange(RECV_SLOTS, dtype=jnp.int32)
-    wanted_slot = owners * per_peer + order_rank
-    matches = (wanted_slot[None, :] == slots_flat[:, None]) & active[None, :]
-    asking = jnp.sum(jnp.where(matches, local_slot[None, :] + 1, 0), axis=1)
-    requests = lax.all_to_all(
-        asking.reshape(devices, per_peer), ("gx", "gy"), split_axis=0, concat_axis=0, tiled=True
-    )
-    wanted = requests.reshape(RECV_SLOTS)
-    block_table = atm_fields.reshape(block_count, block_rows, channels)
-    outgoing = jnp.where(
-        (wanted > 0)[:, None, None],
-        block_table[jnp.maximum(wanted - 1, 0)],
-        jnp.zeros((), jnp.bfloat16),
-    )
-    outgoing = outgoing.reshape(devices, per_peer, block_rows, channels)
-    arrived = lax.all_to_all(outgoing, ("gx", "gy"), split_axis=0, concat_axis=0, tiled=True)
-    arrived = arrived.reshape(RECV_SLOTS, block_rows, channels)
     lat_rows = ocean_state.shape[0]
     lon_cols = ocean_state.shape[1]
     target_blocks = lat_rows * lon_cols // block_rows
-    slots = jnp.where(active, owners * per_peer + order_rank, 0)
-    select = (
-        (tile_tgt[:, None] == jnp.arange(target_blocks, dtype=jnp.int32)[None, :]) & active[:, None]
-    ).astype(jnp.float32)
-    group_size = max((divisor for divisor in range(1, 33) if tiles % divisor == 0))
-    groups = tiles // group_size
-
-    def advance(running, pieces):
-        weights, group_slots, group_select = pieces
-        gathered = arrived[group_slots]
-        partial_sum = jnp.einsum(
-            "tij,tjc->tic", weights, gathered, preferred_element_type=jnp.float32
-        )
-        added = jnp.einsum(
-            "tb,tic->bic", group_select, partial_sum, precision=lax.Precision.HIGHEST
-        )
-        return (running + added, None)
-
-    starting = jnp.zeros((target_blocks, block_rows, channels), jnp.float32)
-    remapped = lax.scan(
-        advance,
-        starting,
-        (
-            tile_weight.reshape(groups, group_size, block_rows, block_rows),
-            slots.reshape(groups, group_size),
-            select.reshape(groups, group_size, target_blocks),
-        ),
-    )[0]
+    block_table = atm_fields.reshape(block_count, block_rows, channels)
+    active = jnp.arange(tiles, dtype=jnp.int32) < tile_count[0]
+    target = jnp.where(active, tile_tgt, target_blocks)
+    if devices * atm_fields.size * atm_fields.dtype.itemsize <= GATHER_LIMIT:
+        place, buffers = gathered_blocks(block_table, atm_pos[tile_src])
+    else:
+        place, buffers = exchanged_blocks(block_table, tile_src, tile_count[0], atm_pos)
+    remapped = remap(place, target, tile_weight, buffers, target_blocks)
     forcing = remapped.reshape(lat_rows, lon_cols, channels)
     mask_half = land_mask.astype(jnp.bfloat16)
     lon_state, lon_mask = (

time: 531 us -> 317 us (0.60)
  starting transfers between devices: 211 us -> 16.7 us
  waiting for transfers between devices: 167 us -> 258 us
  matrix products: 68.1 us -> 0 us
  local copies, waits for them, and re-layouts: 52.5 us -> 4.45 us
  Pallas kernels: 0 us -> 19.8 us
  blocking collectives: 14.3 us -> 0 us
  between operations: 0.89 us -> 14.2 us
  other arithmetic: 16.5 us -> 3.82 us
    all_gather x0 -> x1, waiting for transfers between devices: none -> 249 us  [gathered_blocks(): return (positions, [lax.all_gather(block_table, ('gx', 'gy'), tiled=True)])]
    ppermute x4, starting transfers between devices: 201 us -> 8.31 us  [padded(): before = lax.ppermute(last, axis, up)]
    ppermute x4, waiting for transfers between devices: 87.2 us -> 0.01 us  [padded(): before = lax.ppermute(last, axis, up)]
    all_to_all x1 -> x0, waiting for transfers between devices: 74.2 us -> none  [local(): lax.all_to_all(outgoing, ('gx', 'gy'), split_axis=0, concat_axis=0, tiled...]
    dot_general x10 -> x0, matrix products: 68.1 us -> none  [the longest x5 37.8 us: advance(): jnp.einsum('tb,tic->bic', group_select, partial_sum, precision=lax.Precis...]
    gather x7 -> x1, local copies, waits for them, and re-layouts: 51.2 us -> 1.73 us  [local(): place, buffers = gathered_blocks(block_table, atm_pos[tile_src])]
    pallas_call x0 -> x1, Pallas kernels: none -> 19.8 us  [remap(): pl.pallas_call(body, grid_spec=pltpu.PrefetchScalarGridSpec(num_scalar_pr...]
    all_to_all x1 -> x0, blocking collectives: 14.3 us -> none  [local(): lax.all_to_all(asking.reshape(devices, per_peer), ('gx', 'gy'), split_axi...]
  transfers between devices with their start and end apart: 13 -> 13, of which waited for: 4 -> 4; matrix products, arithmetic and copies ran while one was open for 20% -> 2% of each run, Pallas kernels for 0% -> 6%
where the time goes in v1:
time: 317 us
  waiting for transfers between devices  258 us (81%)
  Pallas kernels  19.8 us (6%)
  starting transfers between devices  16.7 us (5%)
  between operations  14.2 us (4%)
  local copies, waits for them, and re-layouts  4.45 us (1%)
  other arithmetic  3.82 us (1%)
    all_gather x1, waiting for transfers between devices, gathered_blocks(): return (positions, [lax.all_gather(block_table, ('gx', 'gy'), tiled=True)])  249 us
    pallas_call x1, Pallas kernels, remap(): pl.pallas_call(body, grid_spec=pltpu.PrefetchScalarGridSpec(num_scalar_pr...  19.8 us
    ppermute x4, starting transfers between devices, padded(): before = lax.ppermute(last, axis, up)  8.31 us
    ppermute x4, waiting for transfers between devices, padded(): after = lax.ppermute(leading, axis, down)  8.1 us
  transfers between devices with their start and end apart: 13, of which 4 were waited for; matrix products, arithmetic and copies ran while one was open for 2% of the time, Pallas kernels for 6%

profile of v1, /device:TPU:0, one launch (start us, length us, event | category | flops | bytes accessed | tf_op | source)
XLA Modules:
  0.0 316.6 jit_solution(9790392639999838107)
XLA Ops:
  6.5 0.7 all-gather.2.cloned.1.call-update
  7.3 0.7 fusion.17
  8.0 4.9 %collective-permute-start.5 = (bf16[1,32,128]{2,1,0:T(8,128)(2,1)S(1)}, bf16[1,32,128]{2,1,0:T(8,128)(2,1)S(1)}, u32[]{:S(2)}, u32[]{:S(2)}) collective-permute-start(bf16[1,32,128]{2,1,0:T(8,128)(2,1)S(1)} %get-tuple-element.9), channel_id=1, source_target_pairs={{0,1},{1,2},{2,3},{3,4},{4,5},{5,6},{6,7},{8,9},{9,10},{10,11},{11... | collective-permute-start | bytes 24584 | tf_op jit(solution)/shard_map/ppermute | solution.py:89
  12.9 0.8 fusion.18
  13.7 0.7 collective-permute-start.3
  14.4 0.7 fusion.16
  15.1 0.1 rev.8
  15.2 1.0 collective-permute-start.6
  16.2 0.1 fusion.19
  17.0 0.7 compare_select_fusion
  17.7 1.7 gather_fusion
  19.4 1.3 compare_select_fusion.1.target_ref
  20.7 1.7 collective-permute-start.2
  22.4 1.3 collective-permute-done.2
  23.7 3.4 %collective-permute-start.4 = (bf16[1,32]{1,0:T(2,128)(2,1)S(1)}, bf16[1,32]{1,0:T(2,128)(2,1)S(1)}, u32[]{:S(2)}, u32[]{:S(2)}) collective-permute-start(bf16[1,32]{1,0:T(2,128)(2,1)S(1)} %get-tuple-element.17), channel_id=1, source_target_pairs={{0,1},{1,2},{2,3},{3,4},{4,5},{5,6},{6,7},{8,9},{9,10},{10,11},{11... | collective-permute-start | bytes 200 | tf_op jit(solution)/shard_map/ppermute | solution.py:89
  27.2 1.3 collective-permute-start.8
  28.5 0.0 collective-permute-done.4
  28.5 1.2 collective-permute-start.7
  29.7 0.1 fusion.14
  29.7 3.0 collective-permute-done.8
  32.8 0.6 collective-permute-start.9
  33.3 1.3 collective-permute-start.11
  34.6 0.0 collective-permute-done.9
  34.6 0.6 collective-permute-start.10
  35.3 3.8 %collective-permute-done.11 = bf16[1,32,128]{2,1,0:T(8,128)(2,1)S(1)} collective-permute-done((bf16[1,32,128]{2,1,0:T(8,128)(2,1)S(1)}, bf16[1,32,128]{2,1,0:T(8,128)(2,1)S(1)}, u32[]{:S(2)}, u32[]{:S(2)}) %collective-permute-start.11) | collective-permute-done | bytes 8224 | tf_op jit(solution)/shard_map/ppermute | solution.py:90
  39.1 0.0 copy-start.1
  39.1 0.0 slice-start
  39.1 0.0 copy-start.2
  39.1 248.7 %all-gather.2.cloned.1.call-done.refs_0_ = bf16[768,256,128]{2,1,0:T(8,128)(2,1)} async-done(((bf16[24,256,128]{2,1,0:T(8,128)(2,1)}), bf16[768,256,128]{2,1,0:T(8,128)(2,1)}) %all-gather.2.cloned.1.call-update) | async-done | bytes 50331664 | tf_op jit(solution)/shard_map/all_gather | solution.py:136
  287.8 19.8 %shard_map.91 = f32[3,256,128]{2,1,0:T(8,128)} custom-call(s32[160]{0:T(256)} %gather_fusion, s32[160]{0:T(256)} %compare_select_fusion.1.target_ref, bf16[160,256,256]{2,1,0:T(8,128)(2,1)} %weights.1, bf16[768,256,128]{2,1,0:T(8,128)(2,1)} %all-gather.2.cloned.1.call-done.refs_0_), custom_call_target="tpu_custom_call" | custom-call | tf_op jit(solution)/shard_map/pallas_call | solution.py:63
  307.6 1.0 slice.76
  308.7 1.1 fusion.2
  (22 shorter events, 0.1 us)
Async XLA Ops:
  6.5 11.1 %copy-start = (s32[768]{0:T(1024)S(1)}, s32[768]{0:T(1024)}, u32[]{:S(2)}) copy-start(s32[768]{0:T(1024)} %param.10) | copy-start | bytes 9220
  6.5 281.3 %all-gather.2.cloned.1.call-start = ((), (), s32[]{:S(2)}) async-start(), calls=%async_computation | async-start | bytes 51904512 | tf_op jit(solution)/shard_map/all_gather | solution.py:136
  8.0 300.6 %collective-permute-start.5 = (bf16[1,32,128]{2,1,0:T(8,128)(2,1)S(1)}, bf16[1,32,128]{2,1,0:T(8,128)(2,1)S(1)}, u32[]{:S(2)}, u32[]{:S(2)}) collective-permute-start(bf16[1,32,128]{2,1,0:T(8,128)(2,1)S(1)} %get-tuple-element.9), channel_id=1, source_target_pairs={{0,1},{1,2},{2,3},{3,4},{4,5},{5,6},{6,7},{8,9},{9,10},{10,11},{11... | collective-permute-start | bytes 24584 | tf_op jit(solution)/shard_map/ppermute | solution.py:89
  13.7 294.9 %collective-permute-start.3 = (bf16[16,1,128]{2,1,0:T(2,128)(2,1)S(1)}, bf16[16,1,128]{2,1,0:T(2,128)(2,1)S(1)}, u32[]{:S(2)}, u32[]{:S(2)}) collective-permute-start(bf16[16,1,128]{2,1,0:T(2,128)(2,1)S(1)} %get-tuple-element.11), channel_id=1, source_target_pairs={{8,0},{16,8},{24,16},{0,24},{9,1},{17,9},{25,17},{1,25},{10,2},{18... | collective-permute-start | bytes 12296 | tf_op jit(solution)/shard_map/ppermute | solution.py:90
  14.4 294.2 %collective-permute-start.1 = (bf16[16,1,128]{2,1,0:T(2,128)(2,1)S(1)}, bf16[16,1,128]{2,1,0:T(2,128)(2,1)S(1)}, u32[]{:S(2)}, u32[]{:S(2)}) collective-permute-start(bf16[16,1,128]{2,1,0:T(2,128)(2,1)S(1)} %get-tuple-element.10), channel_id=1, source_target_pairs={{0,8},{8,16},{16,24},{24,0},{1,9},{9,17},{17,25},{25,1},{2,10},{10... | collective-permute-start | bytes 12296 | tf_op jit(solution)/shard_map/ppermute | solution.py:89
  15.2 12.0 %collective-permute-start.6 = (bf16[32]{0:T(256)(128)(2,1)S(1)}, bf16[32]{0:T(256)(128)(2,1)S(1)}, u32[]{:S(2)}, u32[]{:S(2)}) collective-permute-start(bf16[32]{0:T(256)(128)(2,1)S(1)} %rev.8), channel_id=1, source_target_pairs={{0,8},{8,0},{16,24},{24,16},{1,9},{9,1},{17,25},{25,17},{2,10},{10... | collective-permute-start | bytes 200 | tf_op jit(solution)/shard_map/ppermute | solution.py:98
  16.3 4.4 %collective-permute-start = (bf16[16,1]{1,0:T(8,128)(2,1)S(1)}, bf16[16,1]{1,0:T(8,128)(2,1)S(1)}, u32[]{:S(2)}, u32[]{:S(2)}) collective-permute-start(bf16[16,1]{1,0:T(8,128)(2,1)S(1)} %get-tuple-element.15), channel_id=1, source_target_pairs={{0,8},{8,16},{16,24},{24,0},{1,9},{9,17},{17,25},{25,1},{2,10},{10... | collective-permute-start | bytes 104 | tf_op jit(solution)/shard_map/ppermute | solution.py:89
  20.7 3.1 collective-permute-start.2
  23.7 4.7 %collective-permute-start.4 = (bf16[1,32]{1,0:T(2,128)(2,1)S(1)}, bf16[1,32]{1,0:T(2,128)(2,1)S(1)}, u32[]{:S(2)}, u32[]{:S(2)}) collective-permute-start(bf16[1,32]{1,0:T(2,128)(2,1)S(1)} %get-tuple-element.17), channel_id=1, source_target_pairs={{0,1},{1,2},{2,3},{3,4},{4,5},{5,6},{6,7},{8,9},{9,10},{10,11},{11... | collective-permute-start | bytes 200 | tf_op jit(solution)/shard_map/ppermute | solution.py:89
  27.2 5.6 %collective-permute-start.8 = (bf16[1,32]{1,0:T(2,128)(2,1)S(1)}, bf16[1,32]{1,0:T(2,128)(2,1)S(1)}, u32[]{:S(2)}, u32[]{:S(2)}) collective-permute-start(bf16[1,32]{1,0:T(2,128)(2,1)S(1)} %get-tuple-element.18), channel_id=1, source_target_pairs={{1,0},{2,1},{3,2},{4,3},{5,4},{6,5},{7,6},{9,8},{10,9},{11,10},{12... | collective-permute-start | bytes 200 | tf_op jit(solution)/shard_map/ppermute | solution.py:90
  28.5 4.9 %collective-permute-start.7 = (bf16[32]{0:T(256)(128)(2,1)S(1)}, bf16[32]{0:T(256)(128)(2,1)S(1)}, u32[]{:S(2)}, u32[]{:S(2)}) collective-permute-start(bf16[32]{0:T(256)(128)(2,1)S(1)} %collective-permute-done.6), channel_id=1, source_target_pairs={{0,16},{8,24},{16,0},{24,8},{1,17},{9,25},{17,1},{25,9},{2,18},{10... | collective-permute-start | bytes 200 | tf_op jit(solution)/shard_map/ppermute | solution.py:98
  32.8 1.9 collective-permute-start.9
  33.3 5.7 %collective-permute-start.11 = (bf16[1,32,128]{2,1,0:T(8,128)(2,1)S(1)}, bf16[1,32,128]{2,1,0:T(8,128)(2,1)S(1)}, u32[]{:S(2)}, u32[]{:S(2)}) collective-permute-start(bf16[1,32,128]{2,1,0:T(8,128)(2,1)S(1)} %get-tuple-element.7), channel_id=1, source_target_pairs={{1,0},{2,1},{3,2},{4,3},{5,4},{6,5},{7,6},{9,8},{10,9},{11,10},{12... | collective-permute-start | bytes 24584 | tf_op jit(solution)/shard_map/ppermute | solution.py:90
  34.6 4.4 %collective-permute-start.10 = (bf16[32,128]{1,0:T(8,128)(2,1)S(1)}, bf16[32,128]{1,0:T(8,128)(2,1)S(1)}, u32[]{:S(2)}, u32[]{:S(2)}) collective-permute-start(bf16[32,128]{1,0:T(8,128)(2,1)S(1)} %collective-permute-done.9), channel_id=1, source_target_pairs={{0,16},{8,24},{16,0},{24,8},{1,17},{9,25},{17,1},{25,9},{2,18},{10... | collective-permute-start | bytes 24584 | tf_op jit(solution)/shard_map/ppermute | solution.py:98
  39.1 269.6 %copy-start.1 = (bf16[16,32,128]{2,1,0:T(8,128)(2,1)S(1)}, bf16[16,32,128]{2,1,0:T(8,128)(2,1)}, u32[]{:S(2)}) copy-start(bf16[16,32,128]{2,1,0:T(8,128)(2,1)} %param.15) | copy-start | bytes 393220
  39.1 269.6 %slice-start = ((bf16[16,32,128]{2,1,0:T(8,128)(2,1)}), bf16[15,32,128]{2,1,0:T(8,128)(2,1)S(1)}, s32[]{:S(2)}) async-start(bf16[16,32,128]{2,1,0:T(8,128)(2,1)} %param.15), calls=%async_computation.1 | async-start | bytes 245760 | tf_op jit(solution)/shard_map/slice | solution.py:174
  39.1 269.6 %copy-start.2 = (f32[128]{0:T(128)S(1)}, f32[128]{0:T(128)}, u32[]{:S(2)}) copy-start(f32[128]{0:T(128)} %param.17) | copy-start | bytes 1540
Sparse Core Ops, SparseCore 0:
  10.2 277.5 all-gather.1
